TPU v7x, 128 devices: a whole 4x4x4 slice. The times are simulated.
128 devices in a mesh: rep: 2 (over y_lo), own: 64 (over x, z, y_hi, core).
Axes of the slice: x: 4, y: 4 (y_hi: 2, y_lo: 2; y = y_hi * 2 + y_lo), z: 4, core: 2. Of those that a mesh axis runs over, the one named last changes fastest.
Arguments:
- values: float32 [1048576, 128], P(('rep', 'own')), may hold values from -0.8 to 0.8
- key_ids: int32 [1048576], P(('rep', 'own')), may hold values from 0 to 262143, as said below
- heavy_ids: int32 [2048], replicated, may hold values from 0 to 262143, as said below
- block_offsets: int32 [128, 64], P(('rep', 'own')), may hold values from 0 to 8191, as said below
- block_counts: int32 [128, 64], P(('rep', 'own')), may hold values from 8 to 64, as said below
Outputs:
- light_sums: float32 [262144, 128], P('own')
- heavy_sums: float32 [2048, 128], P('own')
Inputs may be any that keep to these rules, and one draw needn't show every extreme that they name: `key_ids`: an event in block o of a device has a key in o * 4096 to (o + 1) * 4096 - 1 that is not a heavy key; every event outside all blocks has a heavy key. `heavy_ids`: distinct keys. `block_offsets`: on each device the blocks lie in the order of o, do not meet, and end by position 8192. `block_counts`: at most 64; one owner gets exactly 64 from every device.
All inputs are finite; a program needn't handle non-finite values.
Results may differ from a plain program's by a relative error of at most 0.000075.
Values sent between devices are 32-bit elements; how exact they have to be, the bound alone decides.
No kernel may reach another device: no remote copies, remote signals or barrier semaphores. Data moves between devices by JAX's collectives and lax.ppermute only.
A program may use at most 64 MiB of HBM per device.

v0:
```python
import math
import jax
import jax.numpy as jnp
from jax import lax
from jax.sharding import PartitionSpec as P

KEYS_DEV = 4096
CAP = 64


def over_pieces(x, axis):
    blocks = lax.all_gather(x, axis)
    return blocks.sum(axis=0)


def in_blocks(x, dim, size):
    lengths = x.shape
    blocks = x.reshape(*lengths[:dim], size, lengths[dim] // size, *lengths[dim + 1 :])
    return jnp.moveaxis(blocks, dim, 0)


def sum_at_owner(x, axis, dim):
    size = lax.axis_size(axis)
    blocks = lax.all_to_all(in_blocks(x, dim, size), axis, 0, 0, tiled=True)
    return jnp.sum(blocks, axis=0)


def key_sums(rows_in, row_keys, targets):
    slots = row_keys.shape[0]
    block_len = math.gcd(slots, 2048)
    count_blocks = slots // block_len
    rows_blocks = rows_in.reshape(count_blocks, block_len, rows_in.shape[1])
    keys_blocks = row_keys.reshape(count_blocks, block_len)

    def accumulate(running, pieces):
        rows_piece, keys_piece = pieces
        onehot = (targets[:, None] == keys_piece[None, :]).astype(jnp.float32)
        added = jnp.dot(
            onehot, rows_piece, precision=lax.Precision.HIGHEST, preferred_element_type=jnp.float32
        )
        return (running + added, None)

    start_sums = jnp.zeros((targets.shape[0], rows_in.shape[1]), jnp.float32)
    running, unused = lax.scan(accumulate, start_sums, (rows_blocks, keys_blocks))
    return running


def per_device(values, key_ids, heavy_ids, block_offsets, block_counts):
    owners = lax.axis_size("own")
    pairs = lax.axis_size("rep")
    own_index = lax.axis_index("own")
    rep_index = lax.axis_index("rep")
    width = values.shape[1]
    slot_cap = CAP
    padded_values = jnp.concatenate([values, jnp.zeros((slot_cap, width), jnp.float32)], axis=0)
    padded_keys = jnp.concatenate([key_ids, jnp.full((slot_cap,), -1, jnp.int32)], axis=0)
    slot_iota = jnp.arange(slot_cap, dtype=jnp.int32)
    positions = block_offsets[0][:, None] + slot_iota[None, :]
    valid = slot_iota[None, :] < block_counts[0][:, None]
    block_rows = jnp.where(valid[:, :, None], jnp.take(padded_values, positions, axis=0), 0.0)
    block_keys = jnp.where(valid, jnp.take(padded_keys, positions, axis=0), -1)
    half_keys = KEYS_DEV // 2
    owner_base = (jnp.arange(owners, dtype=jnp.int32) * KEYS_DEV)[:, None]
    which_half = jnp.where(block_keys >= 0, (block_keys - owner_base) // half_keys, -1)
    split_rows = jnp.stack(
        [jnp.where((which_half == side)[:, :, None], block_rows, 0.0) for side in range(pairs)],
        axis=0,
    )
    split_keys = jnp.stack(
        [jnp.where(which_half == side, block_keys, -1) for side in range(pairs)], axis=0
    )
    split_rows = split_rows.reshape(pairs * owners, slot_cap, width)
    split_keys = split_keys.reshape(pairs * owners, slot_cap)
    got_rows, got_keys = (
        lax.all_to_all(split_rows, ("rep", "own"), split_axis=0, concat_axis=0, tiled=True),
        lax.all_to_all(split_keys, ("rep", "own"), split_axis=0, concat_axis=0, tiled=True),
    )
    local_keys = jnp.where(
        got_keys >= 0, got_keys - own_index * KEYS_DEV - rep_index * half_keys, -1
    ).reshape(-1)
    owned_half = key_sums(
        got_rows.reshape(-1, width), local_keys, jnp.arange(half_keys, dtype=jnp.int32)
    )
    light_sums = lax.all_gather(owned_half, "rep", axis=0, tiled=True)
    partial_sums = key_sums(values, key_ids, heavy_ids)
    summed_pair = over_pieces(partial_sums, "rep")
    heavy_sums = sum_at_owner(summed_pair, "own", 0)
    return (light_sums, heavy_sums)


def solution(mesh):
    placed = (
        P(("rep", "own"), None),
        P(("rep", "own")),
        P(),
        P(("rep", "own"), None),
        P(("rep", "own"), None),
    )
    return jax.shard_map(
        per_device,
        mesh=mesh,
        in_specs=placed,
        out_specs=(P("own", None), P("own", None)),
        check_vma=False,
    )
```

profile of v0, /device:TPU:1, one launch (start us, length us, event | category | flops | bytes accessed | tf_op | source)
XLA Modules:
  0.0 223.6 jit_solution(12802448935710163705)
XLA Ops:
  7.2 0.7 compare_select_fusion.2
  8.0 0.8 concatenate.6
  8.8 23.0 %gather_fusion = s32[4096]{0:T(1024)S(1)} fusion(s32[8256]{0:T(1024)S(1)} %concatenate.6, s32[4096]{0:T(1024)S(1)} %broadcast_clamp_fusion), kind=kCustom, calls=%fused_computation | custom fusion | bytes 49152 | tf_op jit(solution)/shard_map/jit(_take)/gather | solution.py:61
  31.9 0.1 compare_select_fusion.5
  32.0 0.6 pad_add_fusion
  32.6 11.5 %all-to-all-start = ((s32[128,1,64]{2,1,0:T(1,128)}), s32[128,1,64]{2,1,0:T(1,128)S(1)}, u32[]{:S(2)}, u32[]{:S(2)}) async-start(s32[128,1,64]{2,1,0:T(1,128)} %bitcast.2), calls=%async_computation | async-start | bytes 131072 | tf_op jit(solution)/shard_map/all_to_all | solution.py:76
  44.2 0.1 broadcast_compare_fusion.1
  44.3 3.7 %concatenate.7 = f32[8256,128]{1,0:T(8,128)} pad(f32[8192,128]{1,0:T(8,128)} %param.9, f32[]{:T(128)} %constant.53.clone.1), padding=0_64x0_0 | pad | bytes 8421380 | tf_op jit(solution)/shard_map/concatenate | solution.py:55
  48.0 13.0 %gather_fusion.1 = f32[4096,128]{1,0:T(8,128)S(1)} fusion(f32[8256,128]{1,0:T(8,128)} %concatenate.7, s32[4096]{0:T(1024)S(1)} %broadcast_clamp_fusion), kind=kCustom, calls=%fused_computation.1 | custom fusion | bytes 4210688 | tf_op jit(solution)/shard_map/jit(_take)/gather | solution.py:60
  61.0 2.5 %fusion.19 = (f32[1,64,64,128]{3,2,1,0:T(8,128)S(1)}, f32[1,64,64,128]{3,2,1,0:T(8,128)S(1)}) fusion(f32[1,64,64,128]{3,2,1,0:T(8,128)S(1)} %bitcast.28, pred[64,64]{1,0:T(8,128)(4,1)S(1)} %get-tuple-element.118, pred[64,64]{1,0:T(8,128)(4,1)S(1)} %get-tuple-element.117, pred[64,64]{1,0:T(8,128)(4,1)S(1)} %get-tuple-element.111, ...), kind=kLoop, calls=%fused_computation.23 | loop fusion | flops 2097152 | bytes 6307840 | tf_op jit(solution)/shard_map/jit(_where)/select_n | solution.py:66
  63.5 2.3 %pad_maximum_fusion = f32[2,64,64,128]{3,2,1,0:T(8,128)} fusion(f32[1,64,64,128]{3,2,1,0:T(8,128)S(1)} %get-tuple-element.114, f32[1,64,64,128]{3,2,1,0:T(8,128)S(1)} %get-tuple-element.113), kind=kLoop, calls=%fused_computation.20 | loop fusion | flops 1048576 | bytes 8388608 | tf_op jit(solution)/shard_map/stack | solution.py:65
  65.8 10.2 %all-to-all-start.1 = ((f32[128,64,128]{2,1,0:T(8,128)}), f32[128,64,128]{2,1,0:T(8,128)}, u32[]{:S(2)}, u32[]{:S(2)}) async-start(f32[128,64,128]{2,1,0:T(8,128)} %bitcast.27), calls=%async_computation.1 | async-start | bytes 8388608 | tf_op jit(solution)/shard_map/all_to_all | solution.py:75
  76.1 34.5 %while.23 = (s32[]{:T(128)}, f32[2048,128]{1,0:T(8,128)S(1)}, s32[2048]{0:T(1024)S(1)}, s32[4,2048]{1,0:T(4,128)S(1)}, f32[4,2048,128]{2,1,0:T(8,128)}, /*index=5*/s32[]{:T(128)}, s32[]{:T(128)}) while((s32[]{:T(128)}, f32[2048,128]{1,0:T(8,128)S(1)}, s32[2048]{0:T(1024)S(1)}, s32[4,2048]{1,0:T(4,128)S(1)}, ...), condition=%wide.region_3.4_spmd.clone, body=%wide.region_2.3_spmd.clone.sunk | while | flops 6447169536 | bytes 3179099 | solution.py:44
  76.1 8.6 %fusion.43 = f32[2048,128]{1,0:T(8,128)S(1)} fusion(s32[2048]{0:T(1024)S(1)} %bitcast.32, s32[2048]{0:T(1024)S(1)} %get-tuple-element.209, f32[2048,128]{1,0:T(8,128)S(1)} %get-tuple-element.201, f32[4,2048,128]{2,1,0:T(8,128)} %get-tuple-element.211, s32[]{:T(128)} %get-tuple-element.200, pred[]{:T(512)S(6)} %compare.33), kind=kOutput, calls=%fused_computation.15.clone.1 | convolution fusion | flops 6447169536 | bytes 3162625 | tf_op jit(solution)/shard_map/while/body/eval_jaxpr/dot_general | solution.py:38
  84.8 8.6 %fusion.43 = f32[2048,128]{1,0:T(8,128)S(1)} fusion(s32[2048]{0:T(1024)S(1)} %bitcast.32, s32[2048]{0:T(1024)S(1)} %get-tuple-element.209, f32[2048,128]{1,0:T(8,128)S(1)} %get-tuple-element.201, f32[4,2048,128]{2,1,0:T(8,128)} %get-tuple-element.211, s32[]{:T(128)} %get-tuple-element.200, pred[]{:T(512)S(6)} %compare.33), kind=kOutput, calls=%fused_computation.15.clone.1 | convolution fusion | flops 6447169536 | bytes 3162625 | tf_op jit(solution)/shard_map/while/body/eval_jaxpr/dot_general | solution.py:38
  93.4 8.6 %fusion.43 = f32[2048,128]{1,0:T(8,128)S(1)} fusion(s32[2048]{0:T(1024)S(1)} %bitcast.32, s32[2048]{0:T(1024)S(1)} %get-tuple-element.209, f32[2048,128]{1,0:T(8,128)S(1)} %get-tuple-element.201, f32[4,2048,128]{2,1,0:T(8,128)} %get-tuple-element.211, s32[]{:T(128)} %get-tuple-element.200, pred[]{:T(512)S(6)} %compare.33), kind=kOutput, calls=%fused_computation.15.clone.1 | convolution fusion | flops 6447169536 | bytes 3162625 | tf_op jit(solution)/shard_map/while/body/eval_jaxpr/dot_general | solution.py:38
  102.0 8.6 %fusion.43 = f32[2048,128]{1,0:T(8,128)S(1)} fusion(s32[2048]{0:T(1024)S(1)} %bitcast.32, s32[2048]{0:T(1024)S(1)} %get-tuple-element.209, f32[2048,128]{1,0:T(8,128)S(1)} %get-tuple-element.201, f32[4,2048,128]{2,1,0:T(8,128)} %get-tuple-element.211, s32[]{:T(128)} %get-tuple-element.200, pred[]{:T(512)S(6)} %compare.33), kind=kOutput, calls=%fused_computation.15.clone.1 | convolution fusion | flops 6447169536 | bytes 3162625 | tf_op jit(solution)/shard_map/while/body/eval_jaxpr/dot_general | solution.py:38
  110.6 1.0 copy-done.1
  111.6 0.2 all-gather.4.cloned.1.call-start
  111.9 0.2 fusion.20
  112.2 17.3 %all-to-all-done.1 = f32[128,64,128]{2,1,0:T(8,128)} async-done(((f32[128,64,128]{2,1,0:T(8,128)}), f32[128,64,128]{2,1,0:T(8,128)}, u32[]{:S(2)}, u32[]{:S(2)}) %all-to-all-start.1) | async-done | bytes 4194336 | tf_op jit(solution)/shard_map/all_to_all | solution.py:75
  129.5 36.5 %while.22 = (s32[]{:T(128)}, f32[2048,128]{1,0:T(8,128)S(1)}, s32[4,2048]{1,0:T(4,128)S(1)}, f32[4,2048,128]{2,1,0:T(8,128)}, s32[]{:T(128)}, /*index=5*/s32[]{:T(128)}) while((s32[]{:T(128)}, f32[2048,128]{1,0:T(8,128)S(1)}, s32[4,2048]{1,0:T(4,128)S(1)}, f32[4,2048,128]{2,1,0:T(8,128)}, s32[]{:T(128)}, /*index=5*/s32[]{:T(128)}) %tuple.48), condition=%wide.region_1.2_spmd.clone, body=%wide.region_0.1_spmd.clone.sunk | while | flops 6447169536 | bytes 3170899 | solution.py:44
  129.5 9.1 %fusion.40 = f32[2048,128]{1,0:T(8,128)S(1)} fusion(s32[2048]{0:T(1024)S(1)} %bitcast.33, f32[2048,128]{1,0:T(8,128)S(1)} %get-tuple-element.182, f32[4,2048,128]{2,1,0:T(8,128)} %get-tuple-element.190, s32[]{:T(128)} %get-tuple-element.181, pred[]{:T(512)S(6)} %compare.32), kind=kOutput, calls=%fused_computation.6.clone.1 | convolution fusion | flops 6447169536 | bytes 3154433 | tf_op jit(solution)/shard_map/while/body/eval_jaxpr/dot_general | solution.py:38
  138.6 9.1 %fusion.40 = f32[2048,128]{1,0:T(8,128)S(1)} fusion(s32[2048]{0:T(1024)S(1)} %bitcast.33, f32[2048,128]{1,0:T(8,128)S(1)} %get-tuple-element.182, f32[4,2048,128]{2,1,0:T(8,128)} %get-tuple-element.190, s32[]{:T(128)} %get-tuple-element.181, pred[]{:T(512)S(6)} %compare.32), kind=kOutput, calls=%fused_computation.6.clone.1 | convolution fusion | flops 6447169536 | bytes 3154433 | tf_op jit(solution)/shard_map/while/body/eval_jaxpr/dot_general | solution.py:38
  147.8 9.1 %fusion.40 = f32[2048,128]{1,0:T(8,128)S(1)} fusion(s32[2048]{0:T(1024)S(1)} %bitcast.33, f32[2048,128]{1,0:T(8,128)S(1)} %get-tuple-element.182, f32[4,2048,128]{2,1,0:T(8,128)} %get-tuple-element.190, s32[]{:T(128)} %get-tuple-element.181, pred[]{:T(512)S(6)} %compare.32), kind=kOutput, calls=%fused_computation.6.clone.1 | convolution fusion | flops 6447169536 | bytes 3154433 | tf_op jit(solution)/shard_map/while/body/eval_jaxpr/dot_general | solution.py:38
  156.9 9.1 %fusion.40 = f32[2048,128]{1,0:T(8,128)S(1)} fusion(s32[2048]{0:T(1024)S(1)} %bitcast.33, f32[2048,128]{1,0:T(8,128)S(1)} %get-tuple-element.182, f32[4,2048,128]{2,1,0:T(8,128)} %get-tuple-element.190, s32[]{:T(128)} %get-tuple-element.181, pred[]{:T(512)S(6)} %compare.32), kind=kOutput, calls=%fused_computation.6.clone.1 | convolution fusion | flops 6447169536 | bytes 3154433 | tf_op jit(solution)/shard_map/while/body/eval_jaxpr/dot_general | solution.py:38
  166.0 1.0 copy-done
  167.0 1.8 reduce_sum.18
  168.9 30.6 %all_to_all.19 = f32[64,32,128]{2,1,0:T(8,128)S(1)} all-to-all(f32[64,32,128]{2,1,0:T(8,128)S(1)} %bitcast.30), channel_id=1, replica_groups=mesh['rep'=2,'own'=64] {'own'}, dimensions={0} | all-to-all | bytes 2097152 | tf_op jit(solution)/shard_map/all_to_all | solution.py:24
  199.4 0.7 reduce_sum.19
  200.1 13.6 %all-gather.4.cloned.1.call-done = f32[4096,128]{1,0:T(8,128)} async-done(((f32[2048,128]{1,0:T(8,128)}), f32[4096,128]{1,0:T(8,128)}) %all-gather.4.cloned.1.call-update) | async-done | bytes 2097168 | tf_op jit(solution)/shard_map/all_gather | solution.py:84
  213.8 3.0 %copy.20 = f32[4096,128]{1,0:T(8,128)} copy(f32[4096,128]{1,0:T(8,128)} %all-gather.4.cloned.1.call-done) | data formatting | bytes 4194304
  (33 shorter events, 0.6 us)
Async XLA Ops:
  8.8 23.1 %copy-start.3 = (s32[1,64]{1,0:T(1,128)S(1)}, s32[1,64]{1,0:T(1,128)}, u32[]{:S(2)}) copy-start(s32[1,64]{1,0:T(1,128)} %param.12) | copy-start | bytes 772
  8.8 23.1 %copy-start.4 = (s32[1,64]{1,0:T(1,128)S(1)}, s32[1,64]{1,0:T(1,128)}, u32[]{:S(2)}) copy-start(s32[1,64]{1,0:T(1,128)} %param.13) | copy-start | bytes 772
  32.6 33.1 %all-to-all-start = ((s32[128,1,64]{2,1,0:T(1,128)}), s32[128,1,64]{2,1,0:T(1,128)S(1)}, u32[]{:S(2)}, u32[]{:S(2)}) async-start(s32[128,1,64]{2,1,0:T(1,128)} %bitcast.2), calls=%async_computation | async-start | bytes 131072 | tf_op jit(solution)/shard_map/all_to_all | solution.py:76
  65.8 10.3 %copy-start.2 = (s32[8192]{0:T(1024)S(1)}, s32[8192]{0:T(1024)}, u32[]{:S(2)}) copy-start(s32[8192]{0:T(1024)} %param.10) | copy-start | bytes 98308
  65.8 10.3 %copy-start.5 = (s32[2048]{0:T(1024)S(1)}, s32[2048]{0:T(1024)}, u32[]{:S(2)}) copy-start(s32[2048]{0:T(1024)} %param.11) | copy-start | bytes 24580
  65.8 63.7 %all-to-all-start.1 = ((f32[128,64,128]{2,1,0:T(8,128)}), f32[128,64,128]{2,1,0:T(8,128)}, u32[]{:S(2)}, u32[]{:S(2)}) async-start(f32[128,64,128]{2,1,0:T(8,128)} %bitcast.27), calls=%async_computation.1 | async-start | bytes 8388608 | tf_op jit(solution)/shard_map/all_to_all | solution.py:75
  76.0 91.0 %all-gather.6.cloned.1.call-start = ((), (), s32[]{:S(2)}) async-start(), calls=%async_computation.4 | async-start | bytes 3145728 | tf_op jit(solution)/shard_map/all_gather | solution.py:12
  110.6 1.0 copy-start.1
  111.6 102.2 %all-gather.4.cloned.1.call-start = ((), (), s32[]{:S(2)}) async-start(), calls=%async_computation.3 | async-start | bytes 3145728 | tf_op jit(solution)/shard_map/all_gather | solution.py:84
  166.0 1.0 copy-start
Sparse Core Ops, SparseCore 0:
  111.7 36.9 all-gather.5
  167.1 46.5 all-gather.3
where the time goes:
time: 224 us
  matrix products  70.7 us (32%)
  local copies, waits for them, and re-layouts  45.9 us (20%)
  waiting for transfers between devices  31 us (14%)
  blocking collectives  30.6 us (14%)
  starting transfers between devices  22 us (10%)
  between operations  14.2 us (6%)
  other arithmetic  9.15 us (4%)
    dot_general x8, matrix products, accumulate(): jnp.dot(onehot, rows_piece, precision=lax.Precision.HIGHEST, preferred_el...  70.7 us
    all_to_all x1, blocking collectives, sum_at_owner(): blocks = lax.all_to_all(in_blocks(x, dim, size), axis, 0, 0, tiled=True)  30.6 us
    gather x3, local copies, waits for them, and re-layouts, per_device(): block_keys = jnp.where(valid, jnp.take(padded_keys, positions, axis=0), -1)  23.2 us
    all_to_all x1, waiting for transfers between devices, per_device(): lax.all_to_all(split_rows, ('rep', 'own'), split_axis=0, concat_axis=0, t...  17.3 us
    all_gather x1, waiting for transfers between devices, per_device(): light_sums = lax.all_gather(owned_half, 'rep', axis=0, tiled=True)  13.6 us
    gather x1, local copies, waits for them, and re-layouts, per_device(): jnp.take(padded_values, positions, axis=0)  13 us
    all_to_all x1, starting transfers between devices, per_device(): lax.all_to_all(split_keys, ('rep', 'own'), split_axis=0, concat_axis=0, t...  11.5 us
    all_to_all x1, starting transfers between devices, per_device(): lax.all_to_all(split_rows, ('rep', 'own'), split_axis=0, concat_axis=0, t...  10.2 us
  transfers between devices with their start and end apart: 4, of which 2 were waited for; matrix products, arithmetic and copies ran while one was open for 43% of the time, Pallas kernels for 0%

commit v1 on v0

--- a/solution.py
+++ b/solution.py
@@ -81,7 +81,9 @@
     owned_half = key_sums(
         got_rows.reshape(-1, width), local_keys, jnp.arange(half_keys, dtype=jnp.int32)
     )
-    light_sums = lax.all_gather(owned_half, "rep", axis=0, tiled=True)
+    light_sums = jnp.concatenate(
+        lax.all_to_all(jnp.stack([owned_half] * lax.axis_size("rep")), "rep", 0, 0), axis=0
+    )
     partial_sums = key_sums(values, key_ids, heavy_ids)
     summed_pair = over_pieces(partial_sums, "rep")
     heavy_sums = sum_at_owner(summed_pair, "own", 0)

time: 224 us -> 238 us (1.062)
  blocking collectives: 30.6 us -> 0 us
  waiting for transfers between devices: 31 us -> 60.5 us
  starting transfers between devices: 22 us -> 36.5 us
  local copies, waits for them, and re-layouts: 45.9 us -> 43.2 us
  other arithmetic: 9.15 us -> 11.6 us
    all_gather x1, waiting for transfers between devices: 0.02 us -> 36.7 us  [over_pieces(): blocks = lax.all_gather(x, axis)]
    all_to_all x1 -> x0, blocking collectives: 30.6 us -> none  [sum_at_owner(): blocks = lax.all_to_all(in_blocks(x, dim, size), axis, 0, 0, tiled=True)]
    all_to_all x0 -> x2, waiting for transfers between devices: none -> 23.7 us  [the longest x1 23.7 us: per_device(): lax.all_to_all(jnp.stack([owned_half] * lax.axis_size('rep')), 'rep', 0, 0)]
    all_to_all x1, waiting for transfers between devices: 17.3 us -> 0.01 us  [per_device(): lax.all_to_all(split_rows, ('rep', 'own'), split_axis=0, concat_axis=0, t...]
    all_to_all x0 -> x2, starting transfers between devices: none -> 14.7 us  [the longest x1 10.9 us: sum_at_owner(): blocks = lax.all_to_all(in_blocks(x, dim, size), axis, 0, 0, tiled=True)]
    all_gather x1 -> x0, waiting for transfers between devices: 13.6 us -> none  [per_device(): light_sums = lax.all_gather(owned_half, 'rep', axis=0, tiled=True)]
    unnamed x13 -> x11, local copies, waits for them, and re-layouts: 5.01 us -> 2.3 us
  transfers between devices with their start and end apart: 4 -> 5, of which waited for: 2 -> 2; matrix products, arithmetic and copies ran while one was open for 43% -> 41% of each run, Pallas kernels for 0% -> 0%
where the time goes in v1:
time: 238 us; the launch traced here: 237 us
  matrix products  70.7 us (30%)
  waiting for transfers between devices  60.5 us (25%)
  local copies, waits for them, and re-layouts  43.2 us (18%)
  starting transfers between devices  36.5 us (15%)
  between operations  14.2 us (6%)
  other arithmetic  11.6 us (5%)
    dot_general x8, matrix products, accumulate(): jnp.dot(onehot, rows_piece, precision=lax.Precision.HIGHEST, preferred_el...  70.7 us
    all_gather x1, waiting for transfers between devices, over_pieces(): blocks = lax.all_gather(x, axis)  36.7 us
    all_to_all x1, waiting for transfers between devices, per_device(): lax.all_to_all(jnp.stack([owned_half] * lax.axis_size('rep')), 'rep', 0, 0)  23.7 us
    gather x3, local copies, waits for them, and re-layouts, per_device(): block_keys = jnp.where(valid, jnp.take(padded_keys, positions, axis=0), -1)  23.2 us
    gather x1, local copies, waits for them, and re-layouts, per_device(): jnp.take(padded_values, positions, axis=0)  13 us
    all_to_all x1, starting transfers between devices, per_device(): lax.all_to_all(split_keys, ('rep', 'own'), split_axis=0, concat_axis=0, t...  11.5 us
    all_to_all x1, starting transfers between devices, sum_at_owner(): blocks = lax.all_to_all(in_blocks(x, dim, size), axis, 0, 0, tiled=True)  10.9 us
    all_to_all x1, starting transfers between devices, per_device(): lax.all_to_all(split_rows, ('rep', 'own'), split_axis=0, concat_axis=0, t...  10.2 us
  transfers between devices with their start and end apart: 5, of which 2 were waited for; matrix products, arithmetic and copies ran while one was open for 41% of the time, Pallas kernels for 0%

profile of v1, /device:TPU:1, one launch (start us, length us, event | category | flops | bytes accessed | tf_op | source)
XLA Modules:
  0.0 236.9 jit_solution(17682818753660597475)
XLA Ops:
  7.2 0.7 compare_select_fusion.2
  8.0 0.8 concatenate.6
  8.8 23.0 %gather_fusion = s32[4096]{0:T(1024)S(1)} fusion(s32[8256]{0:T(1024)S(1)} %concatenate.6, s32[4096]{0:T(1024)S(1)} %broadcast_clamp_fusion), kind=kCustom, calls=%fused_computation | custom fusion | bytes 49152 | tf_op jit(solution)/shard_map/jit(_take)/gather | solution.py:61
  31.9 0.1 compare_select_fusion.5
  32.0 0.6 pad_add_fusion
  32.6 11.5 %all-to-all-start = ((s32[128,1,64]{2,1,0:T(1,128)}), s32[128,1,64]{2,1,0:T(1,128)S(1)}, u32[]{:S(2)}, u32[]{:S(2)}) async-start(s32[128,1,64]{2,1,0:T(1,128)} %bitcast.2), calls=%async_computation | async-start | bytes 131072 | tf_op jit(solution)/shard_map/all_to_all | solution.py:76
  44.2 0.1 broadcast_compare_fusion.1
  44.3 3.7 %concatenate.7 = f32[8256,128]{1,0:T(8,128)} pad(f32[8192,128]{1,0:T(8,128)} %param.9, f32[]{:T(128)} %constant.53.clone.1), padding=0_64x0_0 | pad | bytes 8421380 | tf_op jit(solution)/shard_map/concatenate | solution.py:55
  48.0 13.0 %gather_fusion.1 = f32[4096,128]{1,0:T(8,128)S(1)} fusion(f32[8256,128]{1,0:T(8,128)} %concatenate.7, s32[4096]{0:T(1024)S(1)} %broadcast_clamp_fusion), kind=kCustom, calls=%fused_computation.1 | custom fusion | bytes 4210688 | tf_op jit(solution)/shard_map/jit(_take)/gather | solution.py:60
  61.0 2.5 %fusion.19 = (f32[1,64,64,128]{3,2,1,0:T(8,128)S(1)}, f32[1,64,64,128]{3,2,1,0:T(8,128)S(1)}) fusion(f32[1,64,64,128]{3,2,1,0:T(8,128)S(1)} %bitcast.30, pred[64,64]{1,0:T(8,128)(4,1)S(1)} %get-tuple-element.118, pred[64,64]{1,0:T(8,128)(4,1)S(1)} %get-tuple-element.117, pred[64,64]{1,0:T(8,128)(4,1)S(1)} %get-tuple-element.111, ...), kind=kLoop, calls=%fused_computation.24 | loop fusion | flops 2097152 | bytes 6307840 | tf_op jit(solution)/shard_map/jit(_where)/select_n | solution.py:66
  63.5 2.3 pad_maximum_fusion
  65.8 10.2 %all-to-all-start.1 = ((f32[128,64,128]{2,1,0:T(8,128)}), f32[128,64,128]{2,1,0:T(8,128)}, u32[]{:S(2)}, u32[]{:S(2)}) async-start(f32[128,64,128]{2,1,0:T(8,128)} %bitcast.29), calls=%async_computation.1 | async-start | bytes 8388608 | tf_op jit(solution)/shard_map/all_to_all | solution.py:75
  76.1 34.5 %while.23 = (s32[]{:T(128)}, f32[2048,128]{1,0:T(8,128)S(1)}, s32[2048]{0:T(1024)S(1)}, s32[4,2048]{1,0:T(4,128)S(1)}, f32[4,2048,128]{2,1,0:T(8,128)}, /*index=5*/s32[]{:T(128)}, s32[]{:T(128)}) while((s32[]{:T(128)}, f32[2048,128]{1,0:T(8,128)S(1)}, s32[2048]{0:T(1024)S(1)}, s32[4,2048]{1,0:T(4,128)S(1)}, ...), condition=%wide.region_3.4_spmd.clone, body=%wide.region_2.3_spmd.clone.sunk | while | flops 6447169536 | bytes 3179099 | solution.py:44
  76.2 8.6 %fusion.43 = f32[2048,128]{1,0:T(8,128)S(1)} fusion(s32[2048]{0:T(1024)S(1)} %bitcast.35, s32[2048]{0:T(1024)S(1)} %get-tuple-element.209, f32[2048,128]{1,0:T(8,128)S(1)} %get-tuple-element.201, f32[4,2048,128]{2,1,0:T(8,128)} %get-tuple-element.211, s32[]{:T(128)} %get-tuple-element.200, pred[]{:T(512)S(6)} %compare.33), kind=kOutput, calls=%fused_computation.15.clone.1 | convolution fusion | flops 6447169536 | bytes 3162625 | tf_op jit(solution)/shard_map/while/body/eval_jaxpr/dot_general | solution.py:38
  84.8 8.6 %fusion.43 = f32[2048,128]{1,0:T(8,128)S(1)} fusion(s32[2048]{0:T(1024)S(1)} %bitcast.35, s32[2048]{0:T(1024)S(1)} %get-tuple-element.209, f32[2048,128]{1,0:T(8,128)S(1)} %get-tuple-element.201, f32[4,2048,128]{2,1,0:T(8,128)} %get-tuple-element.211, s32[]{:T(128)} %get-tuple-element.200, pred[]{:T(512)S(6)} %compare.33), kind=kOutput, calls=%fused_computation.15.clone.1 | convolution fusion | flops 6447169536 | bytes 3162625 | tf_op jit(solution)/shard_map/while/body/eval_jaxpr/dot_general | solution.py:38
  93.4 8.6 %fusion.43 = f32[2048,128]{1,0:T(8,128)S(1)} fusion(s32[2048]{0:T(1024)S(1)} %bitcast.35, s32[2048]{0:T(1024)S(1)} %get-tuple-element.209, f32[2048,128]{1,0:T(8,128)S(1)} %get-tuple-element.201, f32[4,2048,128]{2,1,0:T(8,128)} %get-tuple-element.211, s32[]{:T(128)} %get-tuple-element.200, pred[]{:T(512)S(6)} %compare.33), kind=kOutput, calls=%fused_computation.15.clone.1 | convolution fusion | flops 6447169536 | bytes 3162625 | tf_op jit(solution)/shard_map/while/body/eval_jaxpr/dot_general | solution.py:38
  102.0 8.6 %fusion.43 = f32[2048,128]{1,0:T(8,128)S(1)} fusion(s32[2048]{0:T(1024)S(1)} %bitcast.35, s32[2048]{0:T(1024)S(1)} %get-tuple-element.209, f32[2048,128]{1,0:T(8,128)S(1)} %get-tuple-element.201, f32[4,2048,128]{2,1,0:T(8,128)} %get-tuple-element.211, s32[]{:T(128)} %get-tuple-element.200, pred[]{:T(512)S(6)} %compare.33), kind=kOutput, calls=%fused_computation.15.clone.1 | convolution fusion | flops 6447169536 | bytes 3162625 | tf_op jit(solution)/shard_map/while/body/eval_jaxpr/dot_general | solution.py:38
  110.6 1.0 copy-done
  111.6 0.2 fusion.20
  111.9 36.7 %all-gather.3.cloned.1.call-done = f32[4096,128]{1,0:T(8,128)} async-done(((f32[2048,128]{1,0:T(8,128)}), f32[4096,128]{1,0:T(8,128)}) %all-gather.3.cloned.1.call-update) | async-done | bytes 2097168 | tf_op jit(solution)/shard_map/all_gather | solution.py:12
  148.7 2.8 %reduce_sum.18 = f32[2048,128]{1,0:T(8,128)} reduce(f32[2,2048,128]{2,1,0:T(8,128)} %bitcast.33, f32[]{:T(128)} %constant.53.clone.1), dimensions={0}, to_apply=%region_4.5 | reduce | flops 262144 | bytes 3145732 | tf_op jit(solution)/shard_map/reduce_sum | solution.py:13
  151.5 10.9 %all-to-all-start.3 = ((f32[64,32,128]{2,1,0:T(8,128)}), f32[64,32,128]{2,1,0:T(8,128)S(1)}, u32[]{:S(2)}, u32[]{:S(2)}) async-start(f32[64,32,128]{2,1,0:T(8,128)} %bitcast.10), calls=%async_computation.3 | async-start | bytes 2097152 | tf_op jit(solution)/shard_map/all_to_all | solution.py:24
  162.5 36.6 %while.22 = (s32[]{:T(128)}, f32[2048,128]{1,0:T(8,128)S(1)}, s32[4,2048]{1,0:T(4,128)S(1)}, f32[4,2048,128]{2,1,0:T(8,128)}, s32[]{:T(128)}, /*index=5*/s32[]{:T(128)}) while((s32[]{:T(128)}, f32[2048,128]{1,0:T(8,128)S(1)}, s32[4,2048]{1,0:T(4,128)S(1)}, f32[4,2048,128]{2,1,0:T(8,128)}, s32[]{:T(128)}, /*index=5*/s32[]{:T(128)}) %tuple.48), condition=%wide.region_1.2_spmd.clone, body=%wide.region_0.1_spmd.clone.sunk | while | flops 6447169536 | bytes 3170899 | solution.py:44
  162.5 9.1 %fusion.40 = f32[2048,128]{1,0:T(8,128)S(1)} fusion(s32[2048]{0:T(1024)S(1)} %bitcast.36, f32[2048,128]{1,0:T(8,128)S(1)} %get-tuple-element.182, f32[4,2048,128]{2,1,0:T(8,128)} %get-tuple-element.190, s32[]{:T(128)} %get-tuple-element.181, pred[]{:T(512)S(6)} %compare.32), kind=kOutput, calls=%fused_computation.6.clone.1 | convolution fusion | flops 6447169536 | bytes 3154433 | tf_op jit(solution)/shard_map/while/body/eval_jaxpr/dot_general | solution.py:38
  171.6 9.1 %fusion.40 = f32[2048,128]{1,0:T(8,128)S(1)} fusion(s32[2048]{0:T(1024)S(1)} %bitcast.36, f32[2048,128]{1,0:T(8,128)S(1)} %get-tuple-element.182, f32[4,2048,128]{2,1,0:T(8,128)} %get-tuple-element.190, s32[]{:T(128)} %get-tuple-element.181, pred[]{:T(512)S(6)} %compare.32), kind=kOutput, calls=%fused_computation.6.clone.1 | convolution fusion | flops 6447169536 | bytes 3154433 | tf_op jit(solution)/shard_map/while/body/eval_jaxpr/dot_general | solution.py:38
  180.8 9.1 %fusion.40 = f32[2048,128]{1,0:T(8,128)S(1)} fusion(s32[2048]{0:T(1024)S(1)} %bitcast.36, f32[2048,128]{1,0:T(8,128)S(1)} %get-tuple-element.182, f32[4,2048,128]{2,1,0:T(8,128)} %get-tuple-element.190, s32[]{:T(128)} %get-tuple-element.181, pred[]{:T(512)S(6)} %compare.32), kind=kOutput, calls=%fused_computation.6.clone.1 | convolution fusion | flops 6447169536 | bytes 3154433 | tf_op jit(solution)/shard_map/while/body/eval_jaxpr/dot_general | solution.py:38
  189.9 9.1 %fusion.40 = f32[2048,128]{1,0:T(8,128)S(1)} fusion(s32[2048]{0:T(1024)S(1)} %bitcast.36, f32[2048,128]{1,0:T(8,128)S(1)} %get-tuple-element.182, f32[4,2048,128]{2,1,0:T(8,128)} %get-tuple-element.190, s32[]{:T(128)} %get-tuple-element.181, pred[]{:T(512)S(6)} %compare.32), kind=kOutput, calls=%fused_computation.6.clone.1 | convolution fusion | flops 6447169536 | bytes 3154433 | tf_op jit(solution)/shard_map/while/body/eval_jaxpr/dot_general | solution.py:38
  199.0 1.5 pad_maximum_fusion.1
  200.5 3.8 %all-to-all-start.2 = ((f32[2,2048,128]{2,1,0:T(8,128)}), f32[2,2048,128]{2,1,0:T(8,128)S(1)}, u32[]{:S(2)}, u32[]{:S(2)}) async-start(f32[2,2048,128]{2,1,0:T(8,128)} %pad_maximum_fusion.1), calls=%async_computation.2 | async-start | bytes 4194304 | tf_op jit(solution)/shard_map/all_to_all | solution.py:85
  204.3 0.7 reduce_sum.19
  205.0 23.7 %all-to-all-done.2 = f32[2,2048,128]{2,1,0:T(8,128)S(1)} async-done(((f32[2,2048,128]{2,1,0:T(8,128)}), f32[2,2048,128]{2,1,0:T(8,128)S(1)}, u32[]{:S(2)}, u32[]{:S(2)}) %all-to-all-start.2) | async-done | bytes 2097184 | tf_op jit(solution)/shard_map/all_to_all | solution.py:85
  228.7 1.3 copy.20
  (32 shorter events, 0.5 us)
Async XLA Ops:
  8.8 23.1 %copy-start.2 = (s32[1,64]{1,0:T(1,128)S(1)}, s32[1,64]{1,0:T(1,128)}, u32[]{:S(2)}) copy-start(s32[1,64]{1,0:T(1,128)} %param.12) | copy-start | bytes 772
  8.8 23.1 %copy-start.3 = (s32[1,64]{1,0:T(1,128)S(1)}, s32[1,64]{1,0:T(1,128)}, u32[]{:S(2)}) copy-start(s32[1,64]{1,0:T(1,128)} %param.13) | copy-start | bytes 772
  32.6 33.2 %all-to-all-start = ((s32[128,1,64]{2,1,0:T(1,128)}), s32[128,1,64]{2,1,0:T(1,128)S(1)}, u32[]{:S(2)}, u32[]{:S(2)}) async-start(s32[128,1,64]{2,1,0:T(1,128)} %bitcast.2), calls=%async_computation | async-start | bytes 131072 | tf_op jit(solution)/shard_map/all_to_all | solution.py:76
  63.5 2.3 copy-start.1
  65.8 10.3 %copy-start.4 = (s32[2048]{0:T(1024)S(1)}, s32[2048]{0:T(1024)}, u32[]{:S(2)}) copy-start(s32[2048]{0:T(1024)} %param.11) | copy-start | bytes 24580
  65.8 85.7 %all-to-all-start.1 = ((f32[128,64,128]{2,1,0:T(8,128)}), f32[128,64,128]{2,1,0:T(8,128)}, u32[]{:S(2)}, u32[]{:S(2)}) async-start(f32[128,64,128]{2,1,0:T(8,128)} %bitcast.29), calls=%async_computation.1 | async-start | bytes 8388608 | tf_op jit(solution)/shard_map/all_to_all | solution.py:75
  76.1 72.6 %all-gather.3.cloned.1.call-start = ((), (), s32[]{:S(2)}) async-start(), calls=%async_computation.4 | async-start | bytes 3145728 | tf_op jit(solution)/shard_map/all_gather | solution.py:12
  110.6 1.0 copy-start
  151.5 49.0 %all-to-all-start.3 = ((f32[64,32,128]{2,1,0:T(8,128)}), f32[64,32,128]{2,1,0:T(8,128)S(1)}, u32[]{:S(2)}, u32[]{:S(2)}) async-start(f32[64,32,128]{2,1,0:T(8,128)} %bitcast.10), calls=%async_computation.3 | async-start | bytes 2097152 | tf_op jit(solution)/shard_map/all_to_all | solution.py:24
  200.5 28.2 %all-to-all-start.2 = ((f32[2,2048,128]{2,1,0:T(8,128)}), f32[2,2048,128]{2,1,0:T(8,128)S(1)}, u32[]{:S(2)}, u32[]{:S(2)}) async-start(f32[2,2048,128]{2,1,0:T(8,128)} %pad_maximum_fusion.1), calls=%async_computation.2 | async-start | bytes 4194304 | tf_op jit(solution)/shard_map/all_to_all | solution.py:85
Sparse Core Ops, SparseCore 0:
  111.7 36.9 all-gather.2
